TPU v7x, 256 devices: a whole 4x4x8 slice. The times are simulated.
256 devices in a mesh: ctx: 8 (over z), exp: 32 (over x, y, core).
Axes of the slice: x: 4, y: 4, z: 8, core: 2. Of those that a mesh axis runs over, the one named last changes fastest.
Arguments:
- q_latent: bfloat16 [128, 128, 512], P('exp'), may hold values from -7 to 7
- q_rope: bfloat16 [128, 64, 128], P('exp'), may hold values from -84 to 84
- cache_latent: bfloat16 [128, 4096, 512], P('exp', 'ctx'), may hold values from -6 to 6
- cache_rope: bfloat16 [128, 64, 4096], P('exp', None, 'ctx'), may hold values from -6 to 6
- lengths: int32 [128], P('exp'), may hold values from 1024 to 4096
- w_attn_out: bfloat16 [128, 512, 7168], P('ctx', None, 'exp'), may hold values from -0.1875 to 0.1875
- hidden_in: bfloat16 [128, 7168], P(None, 'exp'), may hold values from -6 to 6
- norm_gain: bfloat16 [7168], replicated, may hold values from 0.5 to 8
- w_gate: bfloat16 [32, 7168, 1024], P('exp', None, 'ctx'), may hold values from -0.0625 to 0.0625
- w_up: bfloat16 [32, 7168, 1024], P('exp', None, 'ctx'), may hold values from -0.0625 to 0.0625
- w_down: bfloat16 [32, 1024, 7168], P('exp', 'ctx'), may hold values from -0.1875 to 0.1875
- expert_ids: int32 [128, 8], replicated, may hold values from 0 to 31, all different within a row; in each aligned block of 128 rows (0 to 127, 128 to 255, ...) at most 64 rows name the same one
- gate_weights: float32 [128, 8], replicated, may hold values from 0.1 to 1
Outputs:
- layer_out: bfloat16 [128, 7168], P('exp', 'ctx')
Inputs may be any that keep to these rules, and one draw needn't show every extreme that they name: `expert_ids`: each row names 8 different experts; over all 128 rows no expert is named more than 64 times, a bound that some block reaches.
All inputs are finite; a program needn't handle non-finite values.
Results may differ from a plain program's by a relative error of at most 0.008.
Values may be sent and summed in bfloat16 or wider, within the bound.
A program may use at most 64 MiB of HBM per device.

v0:
```python
import math

import jax
import jax.numpy as jnp
from jax import lax
from jax.sharding import PartitionSpec as P

SOFTMAX_SCALE = 192.0 ** (-0.5)
MASKED = -1e30
EPSILON = 1e-06


def cut_along(array, dim, devices):
    before, after = (array.shape[:dim], array.shape[dim + 1 :])
    return jnp.moveaxis(array.reshape(*before, devices, -1, *after), dim, 0)


def summed_on_arrival(array, axis, dim):
    devices = lax.axis_size(axis)
    blocks = lax.all_to_all(cut_along(array, dim, devices), axis, 0, 0, tiled=True)
    return jnp.sum(blocks, axis=0)


def sent_together(arrays, axis, dim, along):
    widths = [math.prod(a.shape[along:]) for a in arrays]
    both = jnp.concatenate(
        [a.reshape(*a.shape[:along], w) for a, w in zip(arrays, widths)], axis=along
    )
    filled = summed_on_arrival(both, axis, dim)
    blocks = jnp.split(filled, [sum(widths[:k]) for k in range(1, len(widths))], axis=along)
    return tuple(
        (b.reshape(*filled.shape[:along], *a.shape[along:]) for a, b in zip(arrays, blocks))
    )


def copy_for_each(array, axis):
    copies = jnp.broadcast_to(array, (lax.axis_size(axis), *array.shape))
    return lax.all_to_all(copies, axis, split_axis=0, concat_axis=0, tiled=True)


def taken_together(array, axis):
    everything = copy_for_each(array, axis)
    return jnp.sum(everything, axis=0)


def slot_tables(expert_ids, gate_weights, experts, capacity):
    row_count, top_count = expert_ids.shape
    flat_ids = expert_ids.reshape(-1)
    one_hot = (flat_ids[:, None] == jnp.arange(experts, dtype=jnp.int32)[None, :]).astype(jnp.int32)
    before = jnp.cumsum(one_hot, axis=0) - one_hot
    slot_index = jnp.sum(before * one_hot, axis=1)
    target = flat_ids * capacity + slot_index
    owner_row = jnp.arange(row_count * top_count, dtype=jnp.int32) // top_count
    slot_row = jnp.full((experts * capacity,), row_count, jnp.int32).at[target].set(owner_row)
    slot_gate = (
        jnp.zeros((experts * capacity,), jnp.float32).at[target].set(gate_weights.reshape(-1))
    )
    return (slot_row, slot_gate)


def per_device(
    q_latent,
    q_rope,
    cache_latent,
    cache_rope,
    lengths,
    w_attn_out,
    hidden_in,
    norm_gain,
    w_gate,
    w_up,
    w_down,
    expert_ids,
    gate_weights,
):
    ctx_index = lax.axis_index("ctx")
    exp_index = lax.axis_index("exp")
    ctx_count = lax.axis_size("ctx")
    exp_count = lax.axis_size("exp")
    block_len = cache_latent.shape[1]
    positions = ctx_index * block_len + jnp.arange(block_len, dtype=jnp.int32)
    visible = positions[None, :] < lengths[:, None]
    scores = jnp.einsum("rhl,rpl->rhp", q_latent, cache_latent, preferred_element_type=jnp.float32)
    scores = (
        scores + jnp.einsum("rdh,rdp->rhp", q_rope, cache_rope, preferred_element_type=jnp.float32)
    ) * SOFTMAX_SCALE
    scores = jnp.where(visible[:, None, :], scores, MASKED)
    block_max = jnp.max(scores, axis=2)
    weights = jnp.where(visible[:, None, :], jnp.exp(scores - block_max[..., None]), 0.0)
    block_total = jnp.sum(weights, axis=2)
    block_value = jnp.einsum(
        "rhp,rpl->rhl",
        weights.astype(jnp.bfloat16),
        cache_latent,
        preferred_element_type=jnp.float32,
    )
    head_count = w_attn_out.shape[0]
    joint_max = lax.pmax(block_max, "ctx")
    rescale = jnp.exp(block_max - joint_max)
    share_total, share_value = sent_together(
        (block_total * rescale, block_value * rescale[..., None]), "ctx", 1, 2
    )
    attended = (share_value / share_total[..., None]).astype(jnp.bfloat16)
    latent_width = w_attn_out.shape[1]
    flat_weight = w_attn_out.reshape(head_count * latent_width, w_attn_out.shape[2])
    row_piece = lax.all_gather(attended, "exp", axis=0, tiled=True)
    partial_out = jnp.dot(
        row_piece.reshape(row_piece.shape[0], head_count * latent_width),
        flat_weight,
        preferred_element_type=jnp.float32,
    )
    hidden_state = hidden_in.astype(jnp.float32) + taken_together(partial_out, "ctx")
    row_count = hidden_in.shape[0]
    share_width = hidden_in.shape[1]
    model_width = share_width * exp_count
    column_width = model_width // ctx_count
    top_count = expert_ids.shape[1]
    local_experts = w_gate.shape[0]
    experts = exp_count * local_experts
    capacity = min(row_count, 2 * row_count * top_count // experts)
    slot_row, slot_gate = slot_tables(expert_ids, gate_weights, experts, capacity)
    rounded = hidden_state.astype(jnp.bfloat16)
    padded = jnp.concatenate([rounded, jnp.zeros((1, share_width), jnp.bfloat16)], axis=0)
    outbound = padded[slot_row].reshape(experts, capacity, share_width)
    values = lax.all_to_all(outbound, "exp", split_axis=0, concat_axis=2, tiled=True).astype(
        jnp.float32
    )
    mean_square = jnp.mean(values * values, axis=2, keepdims=True)
    normed = (values * lax.rsqrt(mean_square + EPSILON) * norm_gain.astype(jnp.float32)).astype(
        jnp.bfloat16
    )
    gate_part = jnp.einsum("end,edf->enf", normed, w_gate, preferred_element_type=jnp.float32)
    up_part = jnp.einsum("end,edf->enf", normed, w_up, preferred_element_type=jnp.float32)
    active = (jax.nn.silu(gate_part) * up_part).astype(jnp.bfloat16)
    expert_part = jnp.einsum("enf,efd->end", active, w_down, preferred_element_type=jnp.float32)
    local_rows = lax.dynamic_slice_in_dim(
        slot_row, exp_index * local_experts * capacity, local_experts * capacity
    )
    local_gates = lax.dynamic_slice_in_dim(
        slot_gate, exp_index * local_experts * capacity, local_experts * capacity
    )
    weighted = expert_part.reshape(local_experts * capacity, model_width) * local_gates[:, None]
    owner_block = exp_index * share_width // column_width
    offset = exp_index * share_width % column_width
    column_part = summed_on_arrival(weighted, "ctx", 1)
    summed = jax.ops.segment_sum(column_part, local_rows, num_segments=row_count)
    current = lax.dynamic_slice(summed, (0, offset), (row_count, share_width))
    residual = jnp.where(ctx_index == owner_block, hidden_state, 0.0)
    summed = lax.dynamic_update_slice(summed, current + residual, (0, offset))
    layer_out = summed_on_arrival(summed, "exp", 0)
    return layer_out.astype(jnp.bfloat16)


def solution(mesh):
    in_specs = (
        P("exp", None, None),
        P("exp", None, None),
        P("exp", "ctx", None),
        P("exp", None, "ctx"),
        P("exp"),
        P("ctx", None, "exp"),
        P(None, "exp"),
        P(),
        P("exp", None, "ctx"),
        P("exp", None, "ctx"),
        P("exp", "ctx", None),
        P(),
        P(),
    )
    out_specs = P("exp", "ctx")
    return jax.shard_map(
        per_device, mesh=mesh, in_specs=in_specs, out_specs=out_specs, check_vma=False
    )
```

profile of v0, /device:TPU:32, one launch (start us, length us, event | category | flops | bytes accessed | tf_op | source)
XLA Modules:
  0.0 274.3 jit_solution(6442682698349328505)
XLA Ops:
  6.5 0.9 broadcast_compare_fusion
  7.4 0.7 copy-done
  8.1 1.9 fusion.58
  10.1 0.4 fusion.57
  10.5 17.9 %pmax.7 = f32[4,128]{1,0:T(4,128)S(1)} all-reduce(f32[4,128]{1,0:T(4,128)S(1)} %get-tuple-element.7), channel_id=1, replica_groups=mesh['ctx'=8,'exp'=32] {'ctx'}, use_global_device_ids=true, to_apply=%region_6.7 | all-reduce | flops 512 | bytes 4096 | tf_op jit(solution)/shard_map/pmax | solution.py:98
  28.4 0.3 fusion.25
  28.7 1.6 convolution_multiply_fusion
  30.4 0.3 copy.64
  30.6 1.6 maximum_bitcast_fusion
  32.3 34.8 %all_to_all.29 = f32[8,4,16,513]{3,2,1,0:T(8,128)S(1)} all-to-all(f32[8,4,16,513]{3,2,1,0:T(8,128)S(1)} %maximum_bitcast_fusion), channel_id=1, replica_groups=mesh['ctx'=8,'exp'=32] {'ctx'}, dimensions={0} | all-to-all | bytes 2101248 | tf_op jit(solution)/shard_map/all_to_all | solution.py:20
  67.1 0.7 reduce_sum.68
  67.8 0.8 slice_reduce_fusion
  68.6 1.6 fusion.37
  70.3 46.1 %all-gather.2.cloned.1.call-done = bf16[128,16,512]{2,1,0:T(8,128)(2,1)} async-done(((bf16[4,16,512]{2,1,0:T(8,128)(2,1)}), bf16[128,16,512]{2,1,0:T(8,128)(2,1)}) %all-gather.2.cloned.1.call-update) | async-done | bytes 2097168 | tf_op jit(solution)/shard_map/all_gather | solution.py:106
  116.4 5.2 %fusion.11 = f32[128,224]{0,1:T(8,128)S(1)} fusion(bf16[16,512,224]{1,2,0:T(8,128)(2,1)} %param.18, bf16[128,16,512]{2,1,0:T(8,128)(2,1)} %all-gather.2.cloned.1.call-done), kind=kOutput, calls=%fused_computation.21 | convolution fusion | flops 469762048 | bytes 5881856 | tf_op jit(solution)/shard_map/dot_general | solution.py:107
  121.7 1.0 broadcast_in_dim.59
  122.7 7.5 %all-to-all-start.1 = ((f32[8,128,224]{1,2,0:T(8,128)}), f32[8,128,224]{1,2,0:T(8,128)S(1)}, u32[]{:S(2)}, u32[]{:S(2)}) async-start(f32[8,128,224]{1,2,0:T(8,128)} %broadcast_in_dim.59), calls=%async_computation.1 | async-start | bytes 1835008 | tf_op jit(solution)/shard_map/all_to_all | solution.py:38
  130.1 0.1 copy.59
  130.4 0.1 copy.58
  130.5 0.1 mul.116
  130.6 0.1 copy.63
  130.8 9.0 %reduce-window.6 = s32[32,8,128]{2,1,0:T(8,128)S(1)} reduce-window(s32[32,8,128]{2,1,0:T(8,128)S(1)} %fusion.38, s32[]{:T(128)} %constant.34.clone.1), window={size=1x1x128 pad=0_0x0_0x127_0}, to_apply=%region_0.1 | reduce-window | flops 4161536 | bytes 262148 | tf_op jit(solution)/shard_map/reduce-window
  139.9 0.1 copy.61
  140.1 0.1 broadcast_add_fusion
  140.3 4.3 %scatter_custom_fusion = s32[2048]{0:T(1024)S(1)} fusion(s32[1024]{0:T(1024)S(1)} %bitcast.76, s32[1024]{0:T(1024)S(1)} %add_select_fusion, s32[]{:T(128)} %constant.31.clone.1), kind=kCustom, calls=%fused_computation.66 | custom fusion | bytes 8196 | tf_op jit(solution)/shard_map/scatter | solution.py:54
  144.6 10.3 %all-to-all-done.1 = f32[8,128,224]{1,2,0:T(8,128)S(1)} async-done(((f32[8,128,224]{1,2,0:T(8,128)}), f32[8,128,224]{1,2,0:T(8,128)S(1)}, u32[]{:S(2)}, u32[]{:S(2)}) %all-to-all-start.1) | async-done | bytes 917536 | tf_op jit(solution)/shard_map/all_to_all | solution.py:38
  155.0 0.1 copy.68
  155.2 9.0 %gather_fusion = bf16[2048,224]{1,0:T(8,128)(2,1)} fusion(bf16[129,224]{1,0:T(8,128)(2,1)S(1)} %concatenate.14, s32[2048]{0:T(1024)S(1)} %fusion.46), kind=kCustom, calls=%fused_computation | custom fusion | bytes 1843200 | tf_op jit(solution)/shard_map/gather | solution.py:124
  164.2 5.3 %all-to-all-start.2 = ((bf16[32,64,224]{2,1,0:T(8,128)(2,1)}), bf16[32,64,224]{2,1,0:T(8,128)(2,1)S(1)}, u32[]{:S(2)}, u32[]{:S(2)}) async-start(bf16[32,64,224]{2,1,0:T(8,128)(2,1)} %bitcast.71), calls=%async_computation.2 | async-start | bytes 2097152 | tf_op jit(solution)/shard_map/all_to_all | solution.py:125
  169.6 0.1 copy.71
  169.8 4.5 %scatter_custom_fusion.1 = f32[2048]{0:T(1024)S(1)} fusion(s32[1024]{0:T(1024)S(1)} %bitcast.77, f32[1024]{0:T(1024)S(1)} %reshape.230, f32[]{:T(128)} %constant.28.clone.1), kind=kCustom, calls=%fused_computation.63 | custom fusion | bytes 8196 | tf_op jit(solution)/shard_map/scatter | solution.py:56
  174.3 3.9 %copy.72 = bf16[7168,128]{1,0:T(8,128)(2,1)} copy(bf16[7168,128]{0,1:T(8,128)(2,1)} %bitcast.72) | data formatting | bytes 3670016 | tf_op jit(solution)/shard_map/enf,efd->end/dot_general | solution.py:135
  178.3 8.0 %all-to-all-done.2 = bf16[32,64,224]{2,1,0:T(8,128)(2,1)S(1)} async-done(((bf16[32,64,224]{2,1,0:T(8,128)(2,1)}), bf16[32,64,224]{2,1,0:T(8,128)(2,1)S(1)}, u32[]{:S(2)}, u32[]{:S(2)}) %all-to-all-start.2) | async-done | bytes 917536 | tf_op jit(solution)/shard_map/all_to_all | solution.py:125
  186.3 0.3 fusion
  186.7 0.3 fusion.23
  187.0 1.6 copy.69
  188.6 2.6 convert_element_type.70
  191.2 2.0 fusion.7
  193.2 4.4 %multiply_bitcast_fusion = f32[8,64,896]{2,1,0:T(8,128)} fusion(bf16[8,896,128]{2,1,0:T(8,128)(2,1)} %bitcast.69, f32[64]{0:T(128)S(1)} %dynamic_slice.10, bf16[64,7168]{1,0:T(8,128)(2,1)S(1)} %convert_element_type.70, bf16[1,7168,128]{2,1,0:T(8,128)(2,1)} %param.22, f32[64,128]{1,0:T(8,128)S(1)} %fusion.7), kind=kOutput, calls=%fused_computation.15 | convolution fusion | flops 235388928 | bytes 6455552 | tf_op jit(solution)/shard_map/enf,efd->end/dot_general | solution.py:135
  197.6 5.7 %all-to-all-start.3 = ((f32[8,64,896]{2,1,0:T(8,128)}), f32[8,64,896]{2,1,0:T(8,128)}, u32[]{:S(2)}, u32[]{:S(2)}) async-start(f32[8,64,896]{2,1,0:T(8,128)} %multiply_bitcast_fusion), calls=%async_computation.3 | async-start | bytes 3670016 | tf_op jit(solution)/shard_map/all_to_all | solution.py:20
  203.4 45.0 %all-to-all-done.3 = f32[8,64,896]{2,1,0:T(8,128)} async-done(((f32[8,64,896]{2,1,0:T(8,128)}), f32[8,64,896]{2,1,0:T(8,128)}, u32[]{:S(2)}, u32[]{:S(2)}) %all-to-all-start.3) | async-done | bytes 1835040 | tf_op jit(solution)/shard_map/all_to_all | solution.py:20
  248.4 1.6 reduce_sum.71
  250.0 1.2 scatter_custom_fusion.2
  251.2 0.1 select_add_fusion
  251.3 1.1 dynamic_update_slice.3
  252.4 0.1 reshape.207
  252.6 14.2 %all_to_all.30 = f32[32,4,896]{2,1,0:T(4,128)S(1)} all-to-all(f32[32,4,896]{2,1,0:T(4,128)S(1)} %reshape.207), channel_id=1, replica_groups=mesh['ctx'=8,'exp'=32] {'exp'}, dimensions={0} | all-to-all | bytes 917504 | tf_op jit(solution)/shard_map/all_to_all | solution.py:20
  266.7 0.7 reduce_sum.72
  (38 shorter events, 1.0 us)
Async XLA Ops:
  6.5 1.6 copy-start
  6.5 109.9 %all-gather.2.cloned.1.call-start = ((), (), s32[]{:S(2)}) async-start(), calls=%async_computation.5 | async-start | bytes 2162688 | tf_op jit(solution)/shard_map/all_gather | solution.py:106
  8.1 1.9 copy-start.1
  8.1 1.9 copy-start.2
  121.6 8.5 %copy-start.4 = (s32[128,8]{0,1:T(8,128)S(1)}, s32[128,8]{0,1:T(8,128)}, u32[]{:S(2)}) copy-start(s32[128,8]{0,1:T(8,128)} %param.24) | copy-start | bytes 12292
  121.7 9.0 %copy-start.3 = (bf16[128,224]{0,1:T(8,128)(2,1)S(1)}, bf16[128,224]{0,1:T(8,128)(2,1)}, u32[]{:S(2)}) copy-start(bf16[128,224]{0,1:T(8,128)(2,1)} %param.19) | copy-start | bytes 172036
  122.7 32.3 %all-to-all-start.1 = ((f32[8,128,224]{1,2,0:T(8,128)}), f32[8,128,224]{1,2,0:T(8,128)S(1)}, u32[]{:S(2)}, u32[]{:S(2)}) async-start(f32[8,128,224]{1,2,0:T(8,128)} %broadcast_in_dim.59), calls=%async_computation.1 | async-start | bytes 1835008 | tf_op jit(solution)/shard_map/all_to_all | solution.py:38
  164.2 5.3 %copy-start.5 = (bf16[7168]{0:T(1024)(128)(2,1)S(1)}, bf16[7168]{0:T(1024)(128)(2,1)}, u32[]{:S(2)}) copy-start(bf16[7168]{0:T(1024)(128)(2,1)} %param.20) | copy-start | bytes 43012
  164.2 5.4 %copy-start.6 = (f32[128,8]{0,1:T(8,128)S(1)}, f32[128,8]{0,1:T(8,128)}, u32[]{:S(2)}) copy-start(f32[128,8]{0,1:T(8,128)} %param.25) | copy-start | bytes 12292
  164.2 22.1 %all-to-all-start.2 = ((bf16[32,64,224]{2,1,0:T(8,128)(2,1)}), bf16[32,64,224]{2,1,0:T(8,128)(2,1)S(1)}, u32[]{:S(2)}, u32[]{:S(2)}) async-start(bf16[32,64,224]{2,1,0:T(8,128)(2,1)} %bitcast.71), calls=%async_computation.2 | async-start | bytes 2097152 | tf_op jit(solution)/shard_map/all_to_all | solution.py:125
  197.6 50.8 %all-to-all-start.3 = ((f32[8,64,896]{2,1,0:T(8,128)}), f32[8,64,896]{2,1,0:T(8,128)}, u32[]{:S(2)}, u32[]{:S(2)}) async-start(f32[8,64,896]{2,1,0:T(8,128)} %multiply_bitcast_fusion), calls=%async_computation.3 | async-start | bytes 3670016 | tf_op jit(solution)/shard_map/all_to_all | solution.py:20
Sparse Core Ops, SparseCore 0:
  70.4 45.9 all-gather.1
where the time goes:
time: 278 us; the launch traced here: 274 us
  waiting for transfers between devices  109 us (39%)
  blocking collectives  66.8 us (24%)
  local copies, waits for them, and re-layouts  31.5 us (11%)
  other arithmetic  18.8 us (7%)
  starting transfers between devices  18.5 us (7%)
  matrix products  15.5 us (6%)
  between operations  13.7 us (5%)
    all_to_all x2, blocking collectives, summed_on_arrival(): lax.all_to_all(cut_along(array, dim, devices), axis, 0, 0, tiled=True)  49 us
    all_gather x1, waiting for transfers between devices, per_device(): row_piece = lax.all_gather(attended, 'exp', axis=0, tiled=True)  46.1 us
    all_to_all x1, waiting for transfers between devices, summed_on_arrival(): lax.all_to_all(cut_along(array, dim, devices), axis, 0, 0, tiled=True)  45 us
    pmax x1, blocking collectives, per_device(): joint_max = lax.pmax(block_max, 'ctx')  17.9 us
    all_to_all x1, waiting for transfers between devices, copy_for_each(): return lax.all_to_all(copies, axis, split_axis=0, concat_axis=0, tiled=True)  10.3 us
    another operation x3, other arithmetic  9.15 us
    gather x1, local copies, waits for them, and re-layouts, per_device(): outbound = padded[slot_row].reshape(experts, capacity, share_width)  9 us
    all_to_all x1, waiting for transfers between devices, per_device(): lax.all_to_all(outbound, 'exp', split_axis=0, concat_axis=2, tiled=True)  7.98 us
  transfers between devices with their start and end apart: 4, of which 4 were waited for; matrix products, arithmetic and copies ran while one was open for 8% of the time, Pallas kernels for 0%

commit v1 on v0

v1 whole, which is shorter than its diff:
```python
import functools

import jax
import jax.numpy as jnp
from jax import lax
from jax.experimental import pallas as pl
from jax.experimental.pallas import tpu as pltpu
from jax.sharding import PartitionSpec as P

SCALE = 192.0 ** (-0.5)
MASKED = -1e30
EPSILON = 1e-06
MESH = pl.DeviceIdType.MESH
BF = jnp.bfloat16
F32 = jnp.float32
NZ, NX, NY = 8, 4, 4
HALF = 3584
PART = 1792
TOP = pl.ds(0, PART)
BOT = pl.ds(PART, PART)


def dot(a, b, dims=(((1,), (0,)), ((), ()))):
    return lax.dot_general(a, b, dims, preferred_element_type=F32)


def kernel(
    q_hbm, qr_hbm, kc_hbm, kr_hbm, len_ref, wo_hbm, hid_hbm, gain_hbm, wg_hbm, wu_hbm, wd_hbm,
    ids_hbm, gw_hbm, out_ref,
    qv, qrv, kcv, krv, wov, hidv, gainv, wguv, wdv, idsv, gwv,
    vb, st_s, st_r, br, alv, gbuf, gf, ef, es, er, fg, gds, gsel, actf, actp,
    p1, m1, r1, p2, m2, r2, z3s, z3r,
    lsem, psend, precv, bsend, brecv, gsend, grecv, esend, erecv, fsend, frecv,
    hsend, hrecv, ssend, srecv, ksend, krecv, zsend, zrecv,
):
    z = lax.axis_index("ctx")
    e = lax.axis_index("exp")
    core = lax.rem(e, 2)
    p = lax.div(e, 2)
    y = lax.rem(p, NY)
    x = lax.div(p, NY)
    zq, zk = lax.div(z, 2), lax.rem(z, 2)

    def dev(dz=0, dx=0, dy=0, other=False):
        c = (1 - core) if other else core
        xx, yy = lax.rem(x + dx, NX), lax.rem(y + dy, NY)
        return {"ctx": lax.rem(z + dz, NZ), "exp": (xx * NY + yy) * 2 + c}

    barrier = pltpu.get_barrier_semaphore()
    peers = [dev(dz=d) for d in range(1, NZ)]
    peers += [dev(dx=1), dev(dx=3), dev(dy=1), dev(dy=3), dev(other=True)]
    for peer in peers:
        pl.semaphore_signal(barrier, inc=1, device_id=peer, device_id_type=MESH)

    def load(src, dst, k):
        return pltpu.make_async_copy(src, dst, lsem.at[k])

    row_loads = []
    for r in range(4):
        row_loads.append([
            load(q_hbm.at[r], qv.at[r], 4 * r),
            load(kc_hbm.at[r], kcv.at[r], 4 * r + 1),
            load(qr_hbm.at[r], qrv.at[r], 4 * r + 2),
            load(kr_hbm.at[r], krv.at[r], 4 * r + 3),
        ])
        for c in row_loads[r]:
            c.start()
    own = pl.ds(pl.multiple_of(core * 128, 128), 128)
    small_loads = [
        load(ids_hbm, idsv, 16),
        load(gw_hbm, gwv, 17),
        load(gain_hbm, gainv, 18),
        load(hid_hbm, hidv.at[core], 19),
    ]
    big_loads = [
        load(wo_hbm, wov.at[core], 20),
        load(wg_hbm, wguv.at[core, :, pl.ds(0, 224), pl.ds(0, 128)], 21),
        load(wu_hbm, wguv.at[core, :, pl.ds(0, 224), pl.ds(128, 128)], 22),
        load(wd_hbm, wdv.at[own], 23),
    ]
    for c in small_loads + big_loads:
        c.start()
    wguv[:, :, 224:256, :] = jnp.zeros((2, 32, 32, 256), BF)

    pl.semaphore_wait(barrier, len(peers))

    def swap(src, dst, k):
        return pltpu.make_async_remote_copy(
            src_ref=src, dst_ref=dst, send_sem=psend.at[k], recv_sem=precv.at[k],
            device_id=dev(other=True), device_id_type=MESH,
        )

    swaps = [
        swap(hid_hbm, hidv.at[core], 0),
        swap(wo_hbm, wov.at[core], 1),
        swap(wg_hbm, wguv.at[core, :, pl.ds(0, 224), pl.ds(0, 128)], 2),
        swap(wu_hbm, wguv.at[core, :, pl.ds(0, 224), pl.ds(128, 128)], 3),
        swap(wd_hbm, wdv.at[own], 4),
    ]
    for c in swaps:
        c.start()

    def remote(src, dst, ss, rs, device):
        return pltpu.make_async_remote_copy(
            src_ref=src, dst_ref=dst, send_sem=ss, recv_sem=rs,
            device_id=device, device_id_type=MESH,
        )

    def heads_of(zz):
        return pl.ds(pl.multiple_of(zz * 16, 16), 16)

    def value_copy(r, d):
        zz = lax.rem(z + d, NZ)
        return remote(
            vb.at[r, heads_of(zz)], br.at[z, r], bsend.at[r, d - 1], brecv.at[r, d - 1],
            dev(dz=d),
        )

    def stat_copy(d):
        return remote(st_s, st_r.at[z], bsend.at[4, d - 1], brecv.at[4, d - 1], dev(dz=d))

    lane = lax.broadcasted_iota(jnp.int32, (128, 128), 1)
    position = z * 512 + lax.broadcasted_iota(jnp.int32, (128, 512), 1)
    stats = jnp.zeros((128, 128), F32)
    for r in range(4):
        for c in row_loads[r]:
            c.wait()
        keys = kcv[r]
        scores = dot(qv[r], keys, (((1,), (1,)), ((), ())))
        scores = (scores + dot(qrv[r], krv[r], (((0,), (0,)), ((), ())))) * SCALE
        visible = position < len_ref[r]
        scores = jnp.where(visible, scores, MASKED)
        top = jnp.max(scores, axis=1, keepdims=True)
        weights = jnp.where(visible, jnp.exp(scores - top), 0.0)
        total = jnp.sum(weights, axis=1, keepdims=True)
        value = dot(weights.astype(BF), keys)
        held = jnp.maximum(total, 1e-30)
        vb[r] = (value / held).astype(BF)
        lse = jnp.where(total > 0.0, top + jnp.log(held), MASKED)
        stats = jnp.where(lane == r, lse, stats)
        if r == 3:
            st_s[...] = jnp.transpose(stats)[0:8]
            for d in range(1, NZ):
                stat_copy(d).start()
        for d in range(1, NZ):
            value_copy(r, d).start()
        br[z, r] = vb[r, heads_of(z)]
    st_r[z] = st_s[...]

    for c in small_loads:
        c.wait()
    for k in range(2):
        named = jnp.where(idsv[...] == 2 * p + k, gwv[...], 0.0)
        gds[:, 128 * k:128 * k + 128] = jnp.broadcast_to(
            jnp.sum(named, axis=1, keepdims=True), (128, 128)
        )
    for i in range(16):
        gsel[4 * i:4 * i + 4, :] = jnp.where(
            core == 0, gds[8 * i:8 * i + 4, :], gds[8 * i + 4:8 * i + 8, :]
        )

    for d in range(1, NZ):
        stat_copy(d).wait_recv()
    s = st_r[...]
    a = jnp.exp(s - jnp.max(s, axis=0, keepdims=True))
    a = a / jnp.sum(a, axis=0, keepdims=True)
    a = jnp.concatenate([a.reshape(64, 128), jnp.zeros((64, 128), F32)], axis=0)
    alv[...] = jnp.transpose(a)
    mine = alv[heads_of(z), :]
    for r in range(4):
        for d in range(1, NZ):
            value_copy(r, d).wait_recv()
        acc = jnp.zeros((16, 512), F32)
        for b in range(NZ):
            acc = acc + mine[:, 8 * b + r:8 * b + r + 1] * br[b, r].astype(F32)
        gbuf[x, y, r] = acc.astype(BF)

    def gatherer(buf, send, recv):
        def region(h, i1, i2, first, count):
            i1, i2 = lax.rem(i1, 4), lax.rem(i2, 4)
            xx, yy = (i1, i2) if h == 0 else (i2, i1)
            return buf.at[xx, yy, pl.ds(2 * h + first, count)]

        def copy(h, j, c):
            me1, me2 = (x, y) if h == 0 else (y, x)
            step = 1 if c in (0, 2) else 3
            first, count = {0: (0, 2), 1: (0, 2), 2: (0, 1), 3: (1, 1)}[c]
            shift = {0: 0, 1: 0, 2: 3, 3: 1}[c]
            if j == 4:
                ref = region(h, me1 + shift, me2, first, count)
                along_x = h == 0
            else:
                column = {0: 0, 1: 3, 2: 1, 3: 2}[j]
                ref = region(h, me1 + column, me2 + shift, first, count)
                along_x = h == 1
            target = dev(dx=step) if along_x else dev(dy=step)
            return remote(ref, ref, send.at[h, j, c], recv.at[h, j, c], target)

        for h in range(2):
            copy(h, 4, 0).start()
            copy(h, 4, 1).start()
        for h in range(2):
            copy(h, 0, 0).start()
            copy(h, 0, 1).start()
        for h in range(2):
            for c in range(2):
                copy(h, 4, c).wait_recv()
                copy(h, 4, c + 2).start()
                copy(h, 1 + c, 0).start()
                copy(h, 1 + c, 1).start()
        for j in range(3):
            for h in range(2):
                if j == 1:
                    copy(h, 4, 2).wait_recv()
                    copy(h, 4, 3).wait_recv()
                    copy(h, 3, 0).start()
                    copy(h, 3, 1).start()
                for c in range(2):
                    copy(h, j, c).wait_recv()
                    copy(h, j, c + 2).start()
        for h in range(2):
            for c in range(2):
                copy(h, 3, c).wait_recv()
                copy(h, 3, c + 2).start()
        for j in range(4):
            for h in range(2):
                copy(h, j, 2).wait_recv()
                copy(h, j, 3).wait_recv()
        return [copy(h, j, c) for h in range(2) for j in range(5) for c in range(4)]

    drains = [value_copy(r, d) for r in range(4) for d in range(1, NZ)]
    drains += [stat_copy(d) for d in range(1, NZ)]
    drains += gatherer(gbuf, gsend, grecv)

    for i in range(NX):
        rows = gbuf[i].reshape(256, 512).astype(F32)
        for t in range(4):
            gf[t, pl.ds(256 * i, 256), :] = rows[:, 128 * t:128 * t + 128]
    big_loads[0].wait()
    swaps[1].wait()

    def head(h, accs):
        lhs = jnp.concatenate(
            [gf[t, pl.ds(h, 64, stride=16), :] for t in range(4)], axis=1
        ).astype(BF)
        return (accs[0] + dot(lhs, wov[0, h]), accs[1] + dot(lhs, wov[1, h]))

    accs = lax.fori_loop(0, 16, head, (jnp.zeros((64, 224), F32), jnp.zeros((64, 224), F32)))
    for k in range(2):
        es[k] = jnp.concatenate([accs[k], jnp.zeros((64, 32), F32)], axis=1).astype(BF)

    def rows16(q):
        return pl.ds(pl.multiple_of(q * 16, 16), 16)

    def sum_copy(d):
        zz = lax.rem(z + d, NZ)
        return remote(
            es.at[lax.rem(zz, 2), rows16(lax.div(zz, 2))], er.at[z],
            esend.at[d - 1], erecv.at[d - 1], dev(dz=d),
        )

    for d in range(1, NZ):
        sum_copy(d).start()
    drains += [sum_copy(d) for d in range(1, NZ)]
    er[z] = es[zk, rows16(zq)]
    swaps[0].wait()
    hid = hidv[zk, pl.ds(pl.multiple_of(zq * 32, 32), 32), :].astype(F32)
    hid = jnp.concatenate(
        [jnp.where(core == 0, hid[8 * i:8 * i + 4], hid[8 * i + 4:8 * i + 8]) for i in range(4)],
        axis=0,
    )
    hid = jnp.concatenate([hid, jnp.zeros((16, 32), F32)], axis=1)
    for d in range(1, NZ):
        sum_copy(d).wait_recv()
    for b in range(NZ):
        hid = hid + er[b].astype(F32)
    state = hid.astype(BF).astype(F32)
    square = jnp.sum(state * state, axis=1, keepdims=True)
    high = square.astype(BF).astype(F32)
    lanes = lax.broadcasted_iota(jnp.int32, (16, 256), 1)
    state = jnp.where(lanes == 224, high, jnp.where(lanes == 225, square - high, state))
    unit = 2 * zk + lax.div(zq, 2)
    place = pl.ds(pl.multiple_of(16 * lax.rem(zq, 2), 16), 16)
    fg[x, y, unit, place] = state.astype(BF)

    def state_copy(d):
        ref = fg.at[x, y, unit, place]
        return remote(ref, ref, fsend.at[2, d - 1, 0], frecv.at[2, d - 1, 0], dev(dz=d))

    for d in range(1, NZ):
        state_copy(d).start()
    drains += [state_copy(d) for d in range(1, NZ)]
    for d in range(1, NZ):
        state_copy(d).wait_recv()
    drains += gatherer(fg, fsend, frecv)

    for c in big_loads[1:]:
        c.wait()
    for c in swaps[2:]:
        c.wait()

    def block(k, carry):
        h0, h1, tail = carry
        xx, yy, cc = lax.div(k, 8), lax.rem(lax.div(k, 2), 4), lax.rem(k, 2)
        v = fg[xx, yy, pl.ds(2 * cc, 2)].reshape(64, 256).astype(F32)
        tail = tail + v[:, 128:256]
        lhs = (v * gainv[pl.ds(k, 1), :]).astype(BF)
        return (h0 + dot(lhs, wguv[0, k]), h1 + dot(lhs, wguv[1, k]), tail)

    zero = jnp.zeros((64, 256), F32)
    h0, h1, tail = lax.fori_loop(0, 32, block, (zero, zero, jnp.zeros((64, 128), F32)))
    norm = lax.rsqrt((tail[:, 96:97] + tail[:, 97:98]) / 7168.0 + EPSILON)
    parts = []
    for k, h in enumerate((h0, h1)):
        gate, up = h[:, :128] * norm, h[:, 128:] * norm
        parts.append(gate / (1.0 + jnp.exp(-gate)) * up * gsel[:, 128 * k:128 * k + 128])
    active = jnp.concatenate(parts, axis=1)
    actf[...] = active
    for i in range(4):
        for j in range(4):
            actp[16 * j + 4 * i:16 * j + 4 * i + 4, :] = actf[16 * i + 4 * j:16 * i + 4 * j + 4, :]
    lhs = (active.astype(BF), actp[...].astype(BF))

    def scatterer(h, along_x, p_ref, m_ref, r_ref, send, recv):
        me = x if along_x else y

        def at(shift):
            return lax.rem(me + shift, 4)

        def copy(c):
            plus = c in (0, 2, 4)
            src, dst = [
                (p_ref.at[h, at(2), :, TOP], m_ref.at[h, 0]),
                (p_ref.at[h, at(2), :, BOT], m_ref.at[h, 1]),
                (p_ref.at[h, at(1), :, BOT], r_ref.at[h, 0, :, BOT]),
                (p_ref.at[h, at(3), :, TOP], r_ref.at[h, 1, :, TOP]),
                (p_ref.at[h, at(1), :, TOP], r_ref.at[h, 0, :, TOP]),
                (p_ref.at[h, at(3), :, BOT], r_ref.at[h, 1, :, BOT]),
            ][c]
            step = 1 if plus else 3
            target = dev(dx=step) if along_x else dev(dy=step)
            return remote(src, dst, send.at[h, c], recv.at[h, c], target)

        def begin():
            for c in range(4):
                copy(c).start()

        def middle():
            for c, shift, part in ((0, 1, TOP), (1, 3, BOT)):
                copy(c).wait_recv()
                joined = p_ref[h, at(shift), :, part].astype(F32) + m_ref[h, c].astype(F32)
                p_ref[h, at(shift), :, part] = joined.astype(p_ref.dtype)
                copy(4 + c).start()

        def end():
            for c in range(2, 6):
                copy(c).wait_recv()
            return (
                p_ref[h, me].astype(F32) + r_ref[h, 0].astype(F32) + r_ref[h, 1].astype(F32)
            )

        return begin, middle, end, [copy(c) for c in range(6)]

    first = [scatterer(h, h == 0, p1, m1, r1, hsend, hrecv) for h in range(2)]
    second = [scatterer(h, h == 1, p2, m2, r2, ssend, srecv) for h in range(2)]
    for h in range(2):
        for c in range(7):
            cols = pl.ds(h * HALF + 512 * c, 512)
            part = dot(lhs[h], wdv[:, cols]).astype(BF)
            p1[h, :, :, pl.ds(512 * c, 512)] = part.reshape(4, 16, 512)
        first[h][0]()
    for h in range(2):
        first[h][1]()
    for h in range(2):
        joined = first[h][2]()
        for i in range(4):
            p2[h, i] = joined[4 * i:4 * i + 4].astype(p2.dtype)
        second[h][0]()
    for h in range(2):
        second[h][1]()
    for h in range(2):
        joined = second[h][2]()
        for i in range(4):
            z3s[4 * h + i] = joined[:, 896 * i:896 * i + 896].astype(z3s.dtype)
        drains += first[h][3] + second[h][3]

    def last_copy(d):
        zz = lax.rem(z + d, NZ)
        return remote(z3s.at[zz], z3r.at[z], zsend.at[d - 1], zrecv.at[d - 1], dev(dz=d))

    for d in range(1, NZ):
        last_copy(d).start()
    drains += [last_copy(d) for d in range(1, NZ)]
    z3r[z] = z3s[z]

    pieces = []
    for i in range(4):
        pe = 2 * z + i // 2
        rows = fg[
            lax.div(pe, 4), lax.rem(pe, 4), 2 * (i % 2) + lax.div(x, 2),
            pl.ds(pl.multiple_of(16 * lax.rem(x, 2), 16), 16),
        ].astype(F32)
        picked = jnp.zeros((4, 256), F32)
        for j in range(4):
            picked = picked + jnp.where(y == j, rows[4 * j:4 * j + 4], 0.0)
        pieces.append(picked[:, :224])
    result = jnp.concatenate(pieces, axis=1)
    for d in range(1, NZ):
        last_copy(d).wait_recv()
    for b in range(NZ):
        result = result + z3r[b].astype(F32)
    out_ref[...] = result.astype(BF)
    for c in drains:
        c.wait_send()


def per_device(
    q_latent, q_rope, cache_latent, cache_rope, lengths, w_attn_out, hidden_in, norm_gain,
    w_gate, w_up, w_down, expert_ids, gate_weights,
):
    gain = jnp.pad(norm_gain.reshape(32, 224).astype(F32), ((0, 0), (0, 32)))
    anywhere = pl.BlockSpec(memory_space=pl.ANY)
    specs = [anywhere] * 13
    specs[4] = pl.BlockSpec(memory_space=pltpu.SMEM)
    vmem = pltpu.VMEM
    dma = pltpu.SemaphoreType.DMA
    scratch = [
        vmem((4, 128, 512), BF), vmem((4, 64, 128), BF), vmem((4, 512, 512), BF),
        vmem((4, 64, 512), BF), vmem((2, 16, 512, 224), BF), vmem((2, 128, 224), BF),
        vmem((32, 256), F32), vmem((2, 32, 256, 256), BF), vmem((256, 7168), BF),
        vmem((128, 8), jnp.int32), vmem((128, 8), F32),
        vmem((4, 128, 512), BF), vmem((8, 128), F32), vmem((8, 8, 128), F32),
        vmem((8, 4, 16, 512), BF), vmem((128, 128), F32), vmem((4, 4, 4, 16, 512), BF),
        vmem((4, 1024, 128), F32), vmem((8, 128), F32), vmem((2, 64, 256), BF),
        vmem((8, 16, 256), BF), vmem((4, 4, 4, 32, 256), BF), vmem((128, 256), F32),
        vmem((64, 256), F32), vmem((64, 256), F32), vmem((64, 256), F32),
        vmem((2, 4, 16, HALF), BF), vmem((2, 2, 16, PART), BF), vmem((2, 2, 16, HALF), BF),
        vmem((2, 4, 4, HALF), F32), vmem((2, 2, 4, PART), F32), vmem((2, 2, 4, HALF), F32),
        vmem((8, 4, 896), F32), vmem((8, 4, 896), F32),
        dma((24,)), dma((5,)), dma((5,)), dma((5, 7)), dma((5, 7)),
        dma((2, 5, 4)), dma((2, 5, 4)), dma((7,)), dma((7,)), dma((3, 7, 4)), dma((3, 7, 4)),
        dma((2, 6)), dma((2, 6)), dma((2, 6)), dma((2, 6)), dma((1,)), dma((1,)),
        dma((7,)), dma((7,)),
    ]
    return pl.pallas_call(
        kernel,
        out_shape=jax.ShapeDtypeStruct((4, 896), BF),
        in_specs=specs,
        out_specs=pl.BlockSpec(memory_space=pltpu.VMEM),
        scratch_shapes=scratch,
        compiler_params=pltpu.CompilerParams(
            collective_id=0, has_side_effects=True, vmem_limit_bytes=56 * 1024 * 1024
        ),
    )(
        q_latent, q_rope, cache_latent, cache_rope, lengths, w_attn_out, hidden_in, gain,
        w_gate.reshape(32, 224, 128), w_up.reshape(32, 224, 128), w_down.reshape(128, 7168),
        expert_ids, gate_weights,
    )


def solution(mesh):
    in_specs = (
        P("exp", None, None),
        P("exp", None, None),
        P("exp", "ctx", None),
        P("exp", None, "ctx"),
        P("exp"),
        P("ctx", None, "exp"),
        P(None, "exp"),
        P(),
        P("exp", None, "ctx"),
        P("exp", None, "ctx"),
        P("exp", "ctx", None),
        P(),
        P(),
    )
    return jax.shard_map(
        per_device, mesh=mesh, in_specs=in_specs, out_specs=P("exp", "ctx"), check_vma=False
    )
```

time: 278 us -> 112 us (0.40)
  waiting for transfers between devices: 109 us -> 0 us
  Pallas kernels: 0 us -> 97.7 us
  blocking collectives: 66.8 us -> 0 us
  local copies, waits for them, and re-layouts: 31.5 us -> 12.6 us
  starting transfers between devices: 18.5 us -> 0 us
  other arithmetic: 18.8 us -> 0.61 us
  matrix products: 15.5 us -> 0 us
  between operations: 13.7 us -> 0.01 us
    pallas_call x0 -> x1, Pallas kernels: none -> 97.7 us  [per_device(): pl.pallas_call(kernel, out_shape=jax.ShapeDtypeStruct((4, 896), BF), in_s...]
    all_to_all x3 -> x0, waiting for transfers between devices: 63.3 us -> none  [the longest x1 45 us: summed_on_arrival(): lax.all_to_all(cut_along(array, dim, devices), axis, 0, 0, tiled=True)]
    all_to_all x2 -> x0, blocking collectives: 49 us -> none  [summed_on_arrival(): lax.all_to_all(cut_along(array, dim, devices), axis, 0, 0, tiled=True)]
    all_gather x1 -> x0, waiting for transfers between devices: 46.1 us -> none  [per_device(): row_piece = lax.all_gather(attended, 'exp', axis=0, tiled=True)]
    all_to_all x3 -> x0, starting transfers between devices: 18.5 us -> none  [the longest x1 7.47 us: copy_for_each(): return lax.all_to_all(copies, axis, split_axis=0, concat_axis=0, tiled=True)]
    pmax x1 -> x0, blocking collectives: 17.9 us -> none  [per_device(): joint_max = lax.pmax(block_max, 'ctx')]
    dot_general x6 -> x0, matrix products: 15.5 us -> none  [the longest x1 5.24 us: per_device(): jnp.dot(row_piece.reshape(row_piece.shape[0], head_count * latent_width),...]
    unnamed x17 -> x5, local copies, waits for them, and re-layouts: 1.06 us -> 11.8 us
  transfers between devices with their start and end apart: 4 -> 0, of which waited for: 4 -> 0; matrix products, arithmetic and copies ran while one was open for 8% -> 0% of each run, Pallas kernels for 0% -> 0%
where the time goes in v1:
time: 112 us; the launch traced here: 111 us
  Pallas kernels  97.7 us (87%)
  local copies, waits for them, and re-layouts  12.6 us (11%)
    pallas_call x1, Pallas kernels, per_device(): pl.pallas_call(kernel, out_shape=jax.ShapeDtypeStruct((4, 896), BF), in_s...  97.7 us
    unnamed x5, local copies, waits for them, and re-layouts  11.8 us

profile of v1, /device:TPU:32, one launch (start us, length us, event | category | flops | bytes accessed | tf_op | source)
XLA Modules:
  0.0 110.8 jit_solution(17122345620471089816)
XLA Ops:
  0.0 0.8 convert_element_type.6
  0.8 0.6 pad_convert_fusion.gain_hbm
  1.4 1.6 %copy.15.hid_hbm = bf16[128,224]{1,0:T(8,128)(2,1)} copy(bf16[128,224]{0,1:T(8,128)(2,1)} %param.19) | data formatting | bytes 114688 | tf_op args[6]
  3.0 1.4 %copy.16.ids_hbm = s32[128,8]{1,0:T(8,128)} copy(s32[128,8]{0,1:T(8,128)} %param.24) | data formatting | bytes 8192 | tf_op args[11]
  4.4 1.4 %copy.17.gw_hbm = f32[128,8]{1,0:T(8,128)} copy(f32[128,8]{0,1:T(8,128)} %param.25) | data formatting | bytes 8192 | tf_op args[12]
  5.8 6.1 %copy.14.wo_hbm = bf16[16,512,224]{2,1,0:T(8,128)(2,1)} copy(bf16[16,512,224]{1,2,0:T(8,128)(2,1)} %param.18) | data formatting | bytes 7340032 | tf_op args[5]
  11.9 97.7 %shard_map.127 = bf16[4,896]{1,0:T(4,128)(2,1)} custom-call(bf16[4,128,512]{2,1,0:T(8,128)(2,1)} %q_hbm.1, bf16[4,64,128]{2,1,0:T(8,128)(2,1)} %qr_hbm.1, bf16[4,512,512]{2,1,0:T(8,128)(2,1)} %kc_hbm.1, bf16[4,64,512]{2,1,0:T(8,128)(2,1)} %kr_hbm.1, s32[4]{0:T(128)} %len_ref.1, bf16[16,512,224]{2,1,0:T(8,128)(2,1)} %copy.14.wo_hbm, ...), custom_call_target="tpu_custom_call" | custom-call | tf_op jit(solution)/shard_map/pallas_call | solution.py:445
  109.5 1.3 %copy.19 = bf16[4,896]{1,0:T(4,128)(2,1)} copy(bf16[4,896]{1,0:T(4,128)(2,1)} %shard_map.127) | data formatting | bytes 14336

commit v2 on v1

--- a/solution.py
+++ b/solution.py
@@ -18,6 +18,7 @@
 PART = 1792
 TOP = pl.ds(0, PART)
 BOT = pl.ds(PART, PART)
+ACROSS = (((1,), (1,)), ((), ()))
 
 
 def dot(a, b, dims=(((1,), (0,)), ((), ()))):
@@ -28,10 +29,10 @@
     q_hbm, qr_hbm, kc_hbm, kr_hbm, len_ref, wo_hbm, hid_hbm, gain_hbm, wg_hbm, wu_hbm, wd_hbm,
     ids_hbm, gw_hbm, out_ref,
     qv, qrv, kcv, krv, wov, hidv, gainv, wguv, wdv, idsv, gwv,
-    vb, st_s, st_r, br, alv, gbuf, gf, ef, es, er, fg, gds, gsel, actf, actp,
-    p1, m1, r1, p2, m2, r2, z3s, z3r,
-    lsem, psend, precv, bsend, brecv, gsend, grecv, esend, erecv, fsend, frecv,
-    hsend, hrecv, ssend, srecv, ksend, krecv, zsend, zrecv,
+    vb, st_s, st_r, br, bm, bh, mg, alv, gbuf, gf, ef, es, er, fg, gds, gsel, actf, actp,
+    p1, m1, r1, p2, m2, r2, z3s, z3r, gainf, gainp, hidt,
+    lsem, psend, precv, bsend, brecv, gsend, grecv, esend, erecv, fsend, frecv, tsend, trecv,
+    hsend, hrecv, ssend, srecv, zsend, zrecv,
 ):
     z = lax.axis_index("ctx")
     e = lax.axis_index("exp")
@@ -109,15 +110,23 @@
     def heads_of(zz):
         return pl.ds(pl.multiple_of(zz * 16, 16), 16)
 
-    def value_copy(r, d):
-        zz = lax.rem(z + d, NZ)
-        return remote(
-            vb.at[r, heads_of(zz)], br.at[z, r], bsend.at[r, d - 1], brecv.at[r, d - 1],
-            dev(dz=d),
-        )
+    left256, right256 = pl.ds(0, 256), pl.ds(256, 256)
+
+    def value_copy(r, c):
+        src, dst, d = [
+            (vb.at[r, heads_of(lax.rem(z + 1, NZ))], br.at[0, r], 1),
+            (vb.at[r, heads_of(lax.rem(z + 7, NZ))], br.at[1, r], 7),
+            (vb.at[r, heads_of(lax.rem(z + 3, NZ))], bm.at[0, r], 1),
+            (vb.at[r, heads_of(lax.rem(z + 5, NZ))], bm.at[1, r], 7),
+            (vb.at[r, heads_of(lax.rem(z + 4, NZ)), left256], bh.at[0, r], 2),
+            (vb.at[r, heads_of(lax.rem(z + 4, NZ)), right256], bh.at[1, r], 6),
+            (mg.at[0, r], br.at[2, r], 2),
+            (mg.at[1, r], br.at[3, r], 6),
+        ][c]
+        return remote(src, dst, bsend.at[r, c], brecv.at[r, c], dev(dz=d))
 
     def stat_copy(d):
-        return remote(st_s, st_r.at[z], bsend.at[4, d - 1], brecv.at[4, d - 1], dev(dz=d))
+        return remote(st_s, st_r.at[d], bsend.at[4, d], brecv.at[4, d], dev(dz=d))
 
     lane = lax.broadcasted_iota(jnp.int32, (128, 128), 1)
     position = z * 512 + lax.broadcasted_iota(jnp.int32, (128, 512), 1)
@@ -126,7 +135,7 @@
         for c in row_loads[r]:
             c.wait()
         keys = kcv[r]
-        scores = dot(qv[r], keys, (((1,), (1,)), ((), ())))
+        scores = dot(qv[r], keys, ACROSS)
         scores = (scores + dot(qrv[r], krv[r], (((0,), (0,)), ((), ())))) * SCALE
         visible = position < len_ref[r]
         scores = jnp.where(visible, scores, MASKED)
@@ -142,17 +151,22 @@
             st_s[...] = jnp.transpose(stats)[0:8]
             for d in range(1, NZ):
                 stat_copy(d).start()
-        for d in range(1, NZ):
-            value_copy(r, d).start()
-        br[z, r] = vb[r, heads_of(z)]
-    st_r[z] = st_s[...]
+        for c in (2, 3, 4, 5, 0, 1):
+            value_copy(r, c).start()
+    st_r[0] = st_s[...]
 
     for c in small_loads:
         c.wait()
     for k in range(2):
         named = jnp.where(idsv[...] == 2 * p + k, gwv[...], 0.0)
-        gds[:, 128 * k:128 * k + 128] = jnp.broadcast_to(
-            jnp.sum(named, axis=1, keepdims=True), (128, 128)
+        named = jnp.broadcast_to(jnp.sum(named, axis=0, keepdims=True), (128, 128))
+        gds[:, 128 * k:128 * k + 128] = jnp.transpose(named)
+    gain = gainv[...].astype(F32)
+    gainf[...] = gain
+    gain = jnp.concatenate([gainf[pl.ds(t, 8, stride=7), :] for t in range(7)], axis=1)
+    for k in range(4):
+        gainp[8 * k:8 * k + 8, :] = jnp.concatenate(
+            [gain[:, 224 * k:224 * k + 224], jnp.zeros((8, 32), F32)], axis=1
         )
     for i in range(16):
         gsel[4 * i:4 * i + 4, :] = jnp.where(
@@ -166,76 +180,124 @@
     a = a / jnp.sum(a, axis=0, keepdims=True)
     a = jnp.concatenate([a.reshape(64, 128), jnp.zeros((64, 128), F32)], axis=0)
     alv[...] = jnp.transpose(a)
-    mine = alv[heads_of(z), :]
+    share = [alv[heads_of(lax.rem(z + d, NZ)), :] for d in (0, 2, 6)]
+
+    def scaled(which, d, r, block):
+        return share[which][:, 8 * d + r:8 * d + r + 1] * block.astype(F32)
+
     for r in range(4):
-        for d in range(1, NZ):
-            value_copy(r, d).wait_recv()
-        acc = jnp.zeros((16, 512), F32)
-        for b in range(NZ):
-            acc = acc + mine[:, 8 * b + r:8 * b + r + 1] * br[b, r].astype(F32)
+        for c in (2, 3, 4, 5):
+            value_copy(r, c).wait_recv()
+        for k, near, far in ((0, 1, 2), (1, 7, 6)):
+            to = heads_of(lax.rem(z + (6 if k else 2), NZ))
+            joined = scaled(1 + k, 0, r, vb[r, to]) + scaled(1 + k, near, r, bm[k, r])
+            half = scaled(1 + k, far, r, bh[k, r])
+            pad = jnp.zeros((16, 256), F32)
+            joined = joined + jnp.concatenate([half, pad] if k == 0 else [pad, half], axis=1)
+            mg[k, r] = joined.astype(BF)
+            value_copy(r, 6 + k).start()
+
+    def combine(r):
+        for c in (0, 1, 6, 7):
+            value_copy(r, c).wait_recv()
+        acc = scaled(0, 0, r, vb[r, heads_of(z)])
+        acc = acc + scaled(0, 1, r, br[0, r]) + scaled(0, 7, r, br[1, r])
+        acc = acc + br[2, r].astype(F32) + br[3, r].astype(F32)
         gbuf[x, y, r] = acc.astype(BF)
 
-    def gatherer(buf, send, recv):
-        def region(h, i1, i2, first, count):
+    def gatherer(buf, send, recv, x_first, both, forward):
+        def region(g, i1, i2, part):
             i1, i2 = lax.rem(i1, 4), lax.rem(i2, 4)
-            xx, yy = (i1, i2) if h == 0 else (i2, i1)
-            return buf.at[xx, yy, pl.ds(2 * h + first, count)]
-
-        def copy(h, j, c):
-            me1, me2 = (x, y) if h == 0 else (y, x)
+            xx, yy = (i1, i2) if x_first(g) else (i2, i1)
+            return buf.at[(xx, yy) + part]
+
+        def copy(g, j, c):
+            me1, me2 = (x, y) if x_first(g) else (y, x)
             step = 1 if c in (0, 2) else 3
-            first, count = {0: (0, 2), 1: (0, 2), 2: (0, 1), 3: (1, 1)}[c]
+            part = both(g) if c < 2 else forward(g, c - 2)
             shift = {0: 0, 1: 0, 2: 3, 3: 1}[c]
             if j == 4:
-                ref = region(h, me1 + shift, me2, first, count)
-                along_x = h == 0
+                ref = region(g, me1 + shift, me2, part)
+                along_x = x_first(g)
             else:
                 column = {0: 0, 1: 3, 2: 1, 3: 2}[j]
-                ref = region(h, me1 + column, me2 + shift, first, count)
-                along_x = h == 1
+                ref = region(g, me1 + column, me2 + shift, part)
+                along_x = not x_first(g)
             target = dev(dx=step) if along_x else dev(dy=step)
-            return remote(ref, ref, send.at[h, j, c], recv.at[h, j, c], target)
-
-        for h in range(2):
-            copy(h, 4, 0).start()
-            copy(h, 4, 1).start()
-        for h in range(2):
-            copy(h, 0, 0).start()
-            copy(h, 0, 1).start()
-        for h in range(2):
+            return remote(ref, ref, send.at[g, j, c], recv.at[g, j, c], target)
+
+        def place(g, j, i):
+            me1, me2 = (x, y) if x_first(g) else (y, x)
+            i1 = lax.rem(me1 + {0: 0, 1: 3, 2: 1, 3: 2}[j], 4)
+            i2 = lax.rem(me2 + {0: 0, 1: 3, 2: 1, 3: 2}[i], 4)
+            return (i1, i2) if x_first(g) else (i2, i1)
+
+        def launch(g, j):
+            copy(g, j, 0).start()
+            copy(g, j, 1).start()
+
+        def pass_on(g, j):
             for c in range(2):
-                copy(h, 4, c).wait_recv()
-                copy(h, 4, c + 2).start()
-                copy(h, 1 + c, 0).start()
-                copy(h, 1 + c, 1).start()
-        for j in range(3):
-            for h in range(2):
-                if j == 1:
-                    copy(h, 4, 2).wait_recv()
-                    copy(h, 4, 3).wait_recv()
-                    copy(h, 3, 0).start()
-                    copy(h, 3, 1).start()
-                for c in range(2):
-                    copy(h, j, c).wait_recv()
-                    copy(h, j, c + 2).start()
-        for h in range(2):
-            for c in range(2):
-                copy(h, 3, c).wait_recv()
-                copy(h, 3, c + 2).start()
-        for j in range(4):
-            for h in range(2):
-                copy(h, j, 2).wait_recv()
-                copy(h, j, 3).wait_recv()
-        return [copy(h, j, c) for h in range(2) for j in range(5) for c in range(4)]
-
-    drains = [value_copy(r, d) for r in range(4) for d in range(1, NZ)]
+                copy(g, j, c).wait_recv()
+                copy(g, j, c + 2).start()
+                if j == 4:
+                    launch(g, 1 + c)
+
+        def far(g, j):
+            copy(g, j, 2).wait_recv()
+            copy(g, j, 3).wait_recv()
+            if j == 4:
+                launch(g, 3)
+
+        def stage(g, n):
+            if n == 0:
+                launch(g, 4)
+                launch(g, 0)
+                return [(0, 0)]
+            if n == 1:
+                pass_on(g, 4)
+                return [(1, 0), (2, 0)]
+            if n == 2:
+                pass_on(g, 0)
+                return [(0, 1), (0, 2)]
+            if n == 3:
+                far(g, 4)
+                pass_on(g, 1)
+                pass_on(g, 2)
+                return [(3, 0), (1, 1), (1, 2), (2, 1), (2, 2)]
+            if n == 4:
+                pass_on(g, 3)
+                far(g, 0)
+                return [(0, 3), (3, 1), (3, 2)]
+            far(g, 1)
+            far(g, 2)
+            far(g, 3)
+            return [(1, 3), (2, 3), (3, 3)]
+
+        def copies(groups):
+            return [copy(g, j, c) for g in range(groups) for j in range(5) for c in range(4)]
+
+        return stage, place, copies
+
+    drains = [value_copy(r, c) for r in range(4) for c in range(8)]
     drains += [stat_copy(d) for d in range(1, NZ)]
-    drains += gatherer(gbuf, gsend, grecv)
-
-    for i in range(NX):
-        rows = gbuf[i].reshape(256, 512).astype(F32)
-        for t in range(4):
-            gf[t, pl.ds(256 * i, 256), :] = rows[:, 128 * t:128 * t + 128]
+    stage, _, copies = gatherer(
+        gbuf, gsend, grecv, lambda g: g % 2 == 0, lambda g: (g,),
+        lambda g, c: (g, slice(None), (left256, right256)[c]),
+    )
+    for t in range(9):
+        for g in reversed(range(4)):
+            if t == g:
+                combine(g)
+            if 0 <= t - g < 6:
+                stage(g, t - g)
+            if t - g == 5:
+                for i in range(16):
+                    rows = gbuf[i // 4, i % 4, g].astype(F32)
+                    for k in range(4):
+                        gf[k, 64 * i + 16 * g:64 * i + 16 * g + 16, :] = rows[:, 128 * k:128 * k + 128]
+    drains += copies(4)
+
     big_loads[0].wait()
     swaps[1].wait()
 
@@ -243,7 +305,7 @@
         lhs = jnp.concatenate(
             [gf[t, pl.ds(h, 64, stride=16), :] for t in range(4)], axis=1
         ).astype(BF)
-        return (accs[0] + dot(lhs, wov[0, h]), accs[1] + dot(lhs, wov[1, h]))
+        return (accs[0] + dot(lhs, wov[0, h], ACROSS), accs[1] + dot(lhs, wov[1, h], ACROSS))
 
     accs = lax.fori_loop(0, 16, head, (jnp.zeros((64, 224), F32), jnp.zeros((64, 224), F32)))
     for k in range(2):
@@ -264,12 +326,13 @@
     drains += [sum_copy(d) for d in range(1, NZ)]
     er[z] = es[zk, rows16(zq)]
     swaps[0].wait()
-    hid = hidv[zk, pl.ds(pl.multiple_of(zq * 32, 32), 32), :].astype(F32)
+    hid = jnp.concatenate([hidv[zk].astype(F32), jnp.zeros((32, 128), F32)], axis=0)
+    hidt[...] = jnp.transpose(hid)
+    hid = hidt[pl.ds(pl.multiple_of(zq * 32, 32), 32), :]
     hid = jnp.concatenate(
         [jnp.where(core == 0, hid[8 * i:8 * i + 4], hid[8 * i + 4:8 * i + 8]) for i in range(4)],
         axis=0,
     )
-    hid = jnp.concatenate([hid, jnp.zeros((16, 32), F32)], axis=1)
     for d in range(1, NZ):
         sum_copy(d).wait_recv()
     for b in range(NZ):
@@ -285,30 +348,36 @@
 
     def state_copy(d):
         ref = fg.at[x, y, unit, place]
-        return remote(ref, ref, fsend.at[2, d - 1, 0], frecv.at[2, d - 1, 0], dev(dz=d))
+        return remote(ref, ref, tsend.at[d - 1], trecv.at[d - 1], dev(dz=d))
 
     for d in range(1, NZ):
         state_copy(d).start()
     drains += [state_copy(d) for d in range(1, NZ)]
     for d in range(1, NZ):
         state_copy(d).wait_recv()
-    drains += gatherer(fg, fsend, frecv)
-
     for c in big_loads[1:]:
         c.wait()
     for c in swaps[2:]:
         c.wait()
-
-    def block(k, carry):
-        h0, h1, tail = carry
-        xx, yy, cc = lax.div(k, 8), lax.rem(lax.div(k, 2), 4), lax.rem(k, 2)
-        v = fg[xx, yy, pl.ds(2 * cc, 2)].reshape(64, 256).astype(F32)
-        tail = tail + v[:, 128:256]
-        lhs = (v * gainv[pl.ds(k, 1), :]).astype(BF)
-        return (h0 + dot(lhs, wguv[0, k]), h1 + dot(lhs, wguv[1, k]), tail)
-
+    stage, place_of, copies = gatherer(
+        fg, fsend, frecv, lambda g: g == 0, lambda g: (pl.ds(2 * g, 2),),
+        lambda g, c: (2 * g + c,),
+    )
     zero = jnp.zeros((64, 256), F32)
-    h0, h1, tail = lax.fori_loop(0, 32, block, (zero, zero, jnp.zeros((64, 128), F32)))
+    h0, h1, tail = zero, zero, jnp.zeros((64, 128), F32)
+    for n in range(6):
+        blocks = [(g, b) for g in range(2) for b in stage(g, n)]
+        for g, (j, i) in blocks:
+            xx, yy = place_of(g, j, i)
+            k = (xx * NY + yy) * 2 + g
+            v = fg[xx, yy, pl.ds(2 * g, 2)].reshape(64, 256).astype(F32)
+            tail = tail + v[:, 128:256]
+            scale = gainp[pl.ds(8 * lax.rem(k, 4) + lax.div(k, 4), 1), :]
+            lhs = (v * scale).astype(BF)
+            h0 = h0 + dot(lhs, wguv[0, k])
+            h1 = h1 + dot(lhs, wguv[1, k])
+    drains += copies(2)
+
     norm = lax.rsqrt((tail[:, 96:97] + tail[:, 97:98]) / 7168.0 + EPSILON)
     parts = []
     for k, h in enumerate((h0, h1)):
@@ -418,7 +487,6 @@
     q_latent, q_rope, cache_latent, cache_rope, lengths, w_attn_out, hidden_in, norm_gain,
     w_gate, w_up, w_down, expert_ids, gate_weights,
 ):
-    gain = jnp.pad(norm_gain.reshape(32, 224).astype(F32), ((0, 0), (0, 32)))
     anywhere = pl.BlockSpec(memory_space=pl.ANY)
     specs = [anywhere] * 13
     specs[4] = pl.BlockSpec(memory_space=pltpu.SMEM)
@@ -426,20 +494,23 @@
     dma = pltpu.SemaphoreType.DMA
     scratch = [
         vmem((4, 128, 512), BF), vmem((4, 64, 128), BF), vmem((4, 512, 512), BF),
-        vmem((4, 64, 512), BF), vmem((2, 16, 512, 224), BF), vmem((2, 128, 224), BF),
-        vmem((32, 256), F32), vmem((2, 32, 256, 256), BF), vmem((256, 7168), BF),
-        vmem((128, 8), jnp.int32), vmem((128, 8), F32),
+        vmem((4, 64, 512), BF), vmem((2, 16, 224, 512), BF), vmem((2, 224, 128), BF),
+        vmem((56, 128), BF), vmem((2, 32, 256, 256), BF), vmem((256, 7168), BF),
+        vmem((8, 128), jnp.int32), vmem((8, 128), F32),
         vmem((4, 128, 512), BF), vmem((8, 128), F32), vmem((8, 8, 128), F32),
-        vmem((8, 4, 16, 512), BF), vmem((128, 128), F32), vmem((4, 4, 4, 16, 512), BF),
+        vmem((4, 4, 16, 512), BF), vmem((2, 4, 16, 512), BF), vmem((2, 4, 16, 256), BF),
+        vmem((2, 4, 16, 512), BF), vmem((128, 128), F32), vmem((4, 4, 4, 16, 512), BF),
         vmem((4, 1024, 128), F32), vmem((8, 128), F32), vmem((2, 64, 256), BF),
         vmem((8, 16, 256), BF), vmem((4, 4, 4, 32, 256), BF), vmem((128, 256), F32),
         vmem((64, 256), F32), vmem((64, 256), F32), vmem((64, 256), F32),
         vmem((2, 4, 16, HALF), BF), vmem((2, 2, 16, PART), BF), vmem((2, 2, 16, HALF), BF),
-        vmem((2, 4, 4, HALF), F32), vmem((2, 2, 4, PART), F32), vmem((2, 2, 4, HALF), F32),
-        vmem((8, 4, 896), F32), vmem((8, 4, 896), F32),
-        dma((24,)), dma((5,)), dma((5,)), dma((5, 7)), dma((5, 7)),
-        dma((2, 5, 4)), dma((2, 5, 4)), dma((7,)), dma((7,)), dma((3, 7, 4)), dma((3, 7, 4)),
-        dma((2, 6)), dma((2, 6)), dma((2, 6)), dma((2, 6)), dma((1,)), dma((1,)),
+        vmem((2, 4, 4, HALF), BF), vmem((2, 2, 4, PART), BF), vmem((2, 2, 4, HALF), BF),
+        vmem((8, 4, 896), BF), vmem((8, 4, 896), BF), vmem((56, 128), F32),
+        vmem((32, 256), F32), vmem((128, 256), F32),
+        dma((24,)), dma((5,)), dma((5,)), dma((5, 8)), dma((5, 8)),
+        dma((4, 5, 4)), dma((4, 5, 4)), dma((7,)), dma((7,)), dma((2, 5, 4)), dma((2, 5, 4)),
+        dma((7,)), dma((7,)),
+        dma((2, 6)), dma((2, 6)), dma((2, 6)), dma((2, 6)),
         dma((7,)), dma((7,)),
     ]
     return pl.pallas_call(
@@ -452,9 +523,10 @@
             collective_id=0, has_side_effects=True, vmem_limit_bytes=56 * 1024 * 1024
         ),
     )(
-        q_latent, q_rope, cache_latent, cache_rope, lengths, w_attn_out, hidden_in, gain,
+        q_latent, q_rope, cache_latent, cache_rope, lengths, jnp.swapaxes(w_attn_out, 1, 2),
+        hidden_in.T, norm_gain.reshape(56, 128),
         w_gate.reshape(32, 224, 128), w_up.reshape(32, 224, 128), w_down.reshape(128, 7168),
-        expert_ids, gate_weights,
+        expert_ids.T, gate_weights.T,
     )
 
 

time: 112 us -> 95.9 us (0.86)
  local copies, waits for them, and re-layouts: 12.6 us -> 1.29 us
  Pallas kernels: 97.7 us -> 94.4 us
    unnamed x5 -> x1, local copies, waits for them, and re-layouts: 11.8 us -> 1.29 us
    pallas_call x1, Pallas kernels: 97.7 us -> 94.4 us  [per_device(): pl.pallas_call(kernel, out_shape=jax.ShapeDtypeStruct((4, 896), BF), in_s...]
where the time goes in v2:
time: 95.9 us; the launch traced here: 95.7 us
  Pallas kernels  94.4 us (98%)
  local copies, waits for them, and re-layouts  1.29 us (1%)
    pallas_call x1, Pallas kernels, per_device(): pl.pallas_call(kernel, out_shape=jax.ShapeDtypeStruct((4, 896), BF), in_s...  94.4 us

profile of v2, /device:TPU:32, one launch (start us, length us, event | category | flops | bytes accessed | tf_op | source)
XLA Modules:
  0.0 95.7 jit_solution(14473098147328525404)
XLA Ops:
  0.0 94.4 %shard_map.127 = bf16[4,896]{1,0:T(4,128)(2,1)} custom-call(bf16[4,128,512]{2,1,0:T(8,128)(2,1)} %q_hbm.1, bf16[4,64,128]{2,1,0:T(8,128)(2,1)} %qr_hbm.1, bf16[4,512,512]{2,1,0:T(8,128)(2,1)} %kc_hbm.1, bf16[4,64,512]{2,1,0:T(8,128)(2,1)} %kr_hbm.1, s32[4]{0:T(128)} %len_ref.1, bf16[16,224,512]{2,1,0:T(8,128)(2,1)} %bitcast.8, bf16[224,128]{1,0:T(8,128)(2,1)} %bitcast.12, ...), custom_call_target="tpu_custom_call" | custom-call | tf_op jit(solution)/shard_map/pallas_call | solution.py:516
  94.4 1.3 %copy.15 = bf16[4,896]{1,0:T(4,128)(2,1)} copy(bf16[4,896]{1,0:T(4,128)(2,1)} %shard_map.127) | data formatting | bytes 14336

commit v3 on v2

--- a/solution.py
+++ b/solution.py
@@ -15,7 +15,8 @@
 F32 = jnp.float32
 NZ, NX, NY = 8, 4, 4
 HALF = 3584
-PART = 1792
+WIDE = 1792
+PART = 896
 TOP = pl.ds(0, PART)
 BOT = pl.ds(PART, PART)
 ACROSS = (((1,), (1,)), ((), ()))
@@ -253,26 +254,23 @@
             if n == 0:
                 launch(g, 4)
                 launch(g, 0)
-                return [(0, 0)]
-            if n == 1:
+            elif n == 1:
                 pass_on(g, 4)
-                return [(1, 0), (2, 0)]
-            if n == 2:
+            elif n == 2:
                 pass_on(g, 0)
-                return [(0, 1), (0, 2)]
-            if n == 3:
+            elif n == 3:
                 far(g, 4)
                 pass_on(g, 1)
                 pass_on(g, 2)
-                return [(3, 0), (1, 1), (1, 2), (2, 1), (2, 2)]
-            if n == 4:
+            elif n == 4:
                 pass_on(g, 3)
+            elif n == 5:
                 far(g, 0)
-                return [(0, 3), (3, 1), (3, 2)]
-            far(g, 1)
-            far(g, 2)
-            far(g, 3)
-            return [(1, 3), (2, 3), (3, 3)]
+            elif n == 6:
+                far(g, 1)
+                far(g, 2)
+            else:
+                far(g, 3)
 
         def copies(groups):
             return [copy(g, j, c) for g in range(groups) for j in range(5) for c in range(4)]
@@ -281,33 +279,49 @@
 
     drains = [value_copy(r, c) for r in range(4) for c in range(8)]
     drains += [stat_copy(d) for d in range(1, NZ)]
-    stage, _, copies = gatherer(
-        gbuf, gsend, grecv, lambda g: g % 2 == 0, lambda g: (g,),
-        lambda g, c: (g, slice(None), (left256, right256)[c]),
+    stage, place_of, copies = gatherer(
+        gbuf, gsend, grecv, lambda g: g == 0, lambda g: (pl.ds(2 * g, 2),),
+        lambda g, c: (2 * g + c,),
     )
-    for t in range(9):
-        for g in reversed(range(4)):
-            if t == g:
-                combine(g)
-            if 0 <= t - g < 6:
-                stage(g, t - g)
-            if t - g == 5:
-                for i in range(16):
-                    rows = gbuf[i // 4, i % 4, g].astype(F32)
-                    for k in range(4):
-                        gf[k, 64 * i + 16 * g:64 * i + 16 * g + 16, :] = rows[:, 128 * k:128 * k + 128]
-    drains += copies(4)
+
+    def spread(blocks):
+        for g, (j, i) in blocks:
+            xx, yy = place_of(g, j, i)
+            for r in (2 * g, 2 * g + 1):
+                rows = gbuf[xx, yy, r].astype(F32)
+                at = pl.ds(pl.multiple_of((4 * (xx * NY + yy) + r) * 24, 8), 16)
+                for k in range(4):
+                    gf[k, at, :] = rows[:, 128 * k:128 * k + 128]
+
+    def run_gather(stage, use):
+        own = [(0, 0)]
+        for g in range(2):
+            stage(g, 0)
+        use([(g, b) for g in range(2) for b in own])
+        for n, ready in (
+            (1, []), (2, [(1, 0), (2, 0), (0, 1)]), (3, [(0, 2), (3, 0), (1, 1), (1, 2)]),
+            (4, [(2, 1), (2, 2), (3, 1), (3, 2)]), (5, [(0, 3)]), (6, [(1, 3), (2, 3)]),
+            (7, [(3, 3)]),
+        ):
+            for g in range(2):
+                stage(g, n)
+            use([(g, b) for g in range(2) for b in ready])
+
+    for r in range(4):
+        combine(r)
+    run_gather(stage, spread)
+    drains += copies(2)
 
     big_loads[0].wait()
     swaps[1].wait()
 
     def head(h, accs):
         lhs = jnp.concatenate(
-            [gf[t, pl.ds(h, 64, stride=16), :] for t in range(4)], axis=1
+            [gf[t, pl.ds(h, 64, stride=24), :] for t in range(4)], axis=1
         ).astype(BF)
         return (accs[0] + dot(lhs, wov[0, h], ACROSS), accs[1] + dot(lhs, wov[1, h], ACROSS))
 
-    accs = lax.fori_loop(0, 16, head, (jnp.zeros((64, 224), F32), jnp.zeros((64, 224), F32)))
+    accs = lax.fori_loop(0, 16, head, (jnp.zeros((64, 224), F32), jnp.zeros((64, 224), F32)), unroll=4)
     for k in range(2):
         es[k] = jnp.concatenate([accs[k], jnp.zeros((64, 32), F32)], axis=1).astype(BF)
 
@@ -364,18 +378,21 @@
         lambda g, c: (2 * g + c,),
     )
     zero = jnp.zeros((64, 256), F32)
-    h0, h1, tail = zero, zero, jnp.zeros((64, 128), F32)
-    for n in range(6):
-        blocks = [(g, b) for g in range(2) for b in stage(g, n)]
+    sums = [zero, zero, jnp.zeros((64, 128), F32)]
+
+    def multiply(blocks):
         for g, (j, i) in blocks:
             xx, yy = place_of(g, j, i)
             k = (xx * NY + yy) * 2 + g
             v = fg[xx, yy, pl.ds(2 * g, 2)].reshape(64, 256).astype(F32)
-            tail = tail + v[:, 128:256]
             scale = gainp[pl.ds(8 * lax.rem(k, 4) + lax.div(k, 4), 1), :]
             lhs = (v * scale).astype(BF)
-            h0 = h0 + dot(lhs, wguv[0, k])
-            h1 = h1 + dot(lhs, wguv[1, k])
+            sums[0] = sums[0] + dot(lhs, wguv[0, k])
+            sums[1] = sums[1] + dot(lhs, wguv[1, k])
+            sums[2] = sums[2] + v[:, 128:256]
+
+    run_gather(stage, multiply)
+    h0, h1, tail = sums
     drains += copies(2)
 
     norm = lax.rsqrt((tail[:, 96:97] + tail[:, 97:98]) / 7168.0 + EPSILON)
@@ -430,28 +447,29 @@
 
         return begin, middle, end, [copy(c) for c in range(6)]
 
-    first = [scatterer(h, h == 0, p1, m1, r1, hsend, hrecv) for h in range(2)]
-    second = [scatterer(h, h == 1, p2, m2, r2, ssend, srecv) for h in range(2)]
-    for h in range(2):
+    groups = range(4)
+    first = [scatterer(g, g % 2 == 0, p1, m1, r1, hsend, hrecv) for g in groups]
+    second = [scatterer(g, g % 2 == 1, p2, m2, r2, ssend, srecv) for g in groups]
+    for g in groups:
+        base = (g % 2) * HALF + (g // 2) * WIDE
         for c in range(7):
-            cols = pl.ds(h * HALF + 512 * c, 512)
-            part = dot(lhs[h], wdv[:, cols]).astype(BF)
-            p1[h, :, :, pl.ds(512 * c, 512)] = part.reshape(4, 16, 512)
-        first[h][0]()
-    for h in range(2):
-        first[h][1]()
-    for h in range(2):
-        joined = first[h][2]()
+            part = dot(lhs[g % 2], wdv[:, base + 256 * c:base + 256 * c + 256]).astype(BF)
+            p1[g, :, :, 256 * c:256 * c + 256] = part.reshape(4, 16, 256)
+        first[g][0]()
+    for g in groups:
+        first[g][1]()
+    for g in groups:
+        joined = first[g][2]()
         for i in range(4):
-            p2[h, i] = joined[4 * i:4 * i + 4].astype(p2.dtype)
-        second[h][0]()
-    for h in range(2):
-        second[h][1]()
-    for h in range(2):
-        joined = second[h][2]()
-        for i in range(4):
-            z3s[4 * h + i] = joined[:, 896 * i:896 * i + 896].astype(z3s.dtype)
-        drains += first[h][3] + second[h][3]
+            p2[g, i] = joined[4 * i:4 * i + 4].astype(p2.dtype)
+        second[g][0]()
+    for g in groups:
+        second[g][1]()
+    for g in groups:
+        joined = second[g][2]()
+        for i in range(2):
+            z3s[(g % 2) * 4 + (g // 2) * 2 + i] = joined[:, 896 * i:896 * i + 896].astype(z3s.dtype)
+        drains += first[g][3] + second[g][3]
 
     def last_copy(d):
         zz = lax.rem(z + d, NZ)
@@ -500,17 +518,17 @@
         vmem((4, 128, 512), BF), vmem((8, 128), F32), vmem((8, 8, 128), F32),
         vmem((4, 4, 16, 512), BF), vmem((2, 4, 16, 512), BF), vmem((2, 4, 16, 256), BF),
         vmem((2, 4, 16, 512), BF), vmem((128, 128), F32), vmem((4, 4, 4, 16, 512), BF),
-        vmem((4, 1024, 128), F32), vmem((8, 128), F32), vmem((2, 64, 256), BF),
+        vmem((4, 1536, 128), F32), vmem((8, 128), F32), vmem((2, 64, 256), BF),
         vmem((8, 16, 256), BF), vmem((4, 4, 4, 32, 256), BF), vmem((128, 256), F32),
         vmem((64, 256), F32), vmem((64, 256), F32), vmem((64, 256), F32),
-        vmem((2, 4, 16, HALF), BF), vmem((2, 2, 16, PART), BF), vmem((2, 2, 16, HALF), BF),
-        vmem((2, 4, 4, HALF), BF), vmem((2, 2, 4, PART), BF), vmem((2, 2, 4, HALF), BF),
+        vmem((4, 4, 16, WIDE), BF), vmem((4, 2, 16, PART), BF), vmem((4, 2, 16, WIDE), BF),
+        vmem((4, 4, 4, WIDE), BF), vmem((4, 2, 4, PART), BF), vmem((4, 2, 4, WIDE), BF),
         vmem((8, 4, 896), BF), vmem((8, 4, 896), BF), vmem((56, 128), F32),
         vmem((32, 256), F32), vmem((128, 256), F32),
         dma((24,)), dma((5,)), dma((5,)), dma((5, 8)), dma((5, 8)),
-        dma((4, 5, 4)), dma((4, 5, 4)), dma((7,)), dma((7,)), dma((2, 5, 4)), dma((2, 5, 4)),
+        dma((2, 5, 4)), dma((2, 5, 4)), dma((7,)), dma((7,)), dma((2, 5, 4)), dma((2, 5, 4)),
         dma((7,)), dma((7,)),
-        dma((2, 6)), dma((2, 6)), dma((2, 6)), dma((2, 6)),
+        dma((4, 6)), dma((4, 6)), dma((4, 6)), dma((4, 6)),
         dma((7,)), dma((7,)),
     ]
     return pl.pallas_call(

time: 95.9 us -> 89.7 us (0.935)
  Pallas kernels: 94.4 us -> 88.2 us
    pallas_call x1, Pallas kernels: 94.4 us -> 88.2 us  [per_device(): pl.pallas_call(kernel, out_shape=jax.ShapeDtypeStruct((4, 896), BF), in_s...]
where the time goes in v3:
time: 89.7 us; the launch traced here: 89.5 us
  Pallas kernels  88.2 us (98%)
  local copies, waits for them, and re-layouts  1.29 us (1%)
    pallas_call x1, Pallas kernels, per_device(): pl.pallas_call(kernel, out_shape=jax.ShapeDtypeStruct((4, 896), BF), in_s...  88.2 us

profile of v3, /device:TPU:32, one launch (start us, length us, event | category | flops | bytes accessed | tf_op | source)
XLA Modules:
  0.0 89.5 jit_solution(544747271153866644)
XLA Ops:
  0.0 88.2 %shard_map.127 = bf16[4,896]{1,0:T(4,128)(2,1)} custom-call(bf16[4,128,512]{2,1,0:T(8,128)(2,1)} %q_hbm.1, bf16[4,64,128]{2,1,0:T(8,128)(2,1)} %qr_hbm.1, bf16[4,512,512]{2,1,0:T(8,128)(2,1)} %kc_hbm.1, bf16[4,64,512]{2,1,0:T(8,128)(2,1)} %kr_hbm.1, s32[4]{0:T(128)} %len_ref.1, bf16[16,224,512]{2,1,0:T(8,128)(2,1)} %bitcast.8, bf16[224,128]{1,0:T(8,128)(2,1)} %bitcast.12, ...), custom_call_target="tpu_custom_call" | custom-call | tf_op jit(solution)/shard_map/pallas_call | solution.py:534
  88.2 1.3 %copy.15 = bf16[4,896]{1,0:T(4,128)(2,1)} copy(bf16[4,896]{1,0:T(4,128)(2,1)} %shard_map.127) | data formatting | bytes 14336

commit v4 on v3

--- a/solution.py
+++ b/solution.py
@@ -31,7 +31,7 @@
     ids_hbm, gw_hbm, out_ref,
     qv, qrv, kcv, krv, wov, hidv, gainv, wguv, wdv, idsv, gwv,
     vb, st_s, st_r, br, bm, bh, mg, alv, gbuf, gf, ef, es, er, fg, gds, gsel, actf, actp,
-    p1, m1, r1, p2, m2, r2, z3s, z3r, gainf, gainp, hidt,
+    p1, m1, r1, p2, r2, z3s, z3r, gainf, gainp, hidt,
     lsem, psend, precv, bsend, brecv, gsend, grecv, esend, erecv, fsend, frecv, tsend, trecv,
     hsend, hrecv, ssend, srecv, zsend, zrecv,
 ):
@@ -50,7 +50,8 @@
 
     barrier = pltpu.get_barrier_semaphore()
     peers = [dev(dz=d) for d in range(1, NZ)]
-    peers += [dev(dx=1), dev(dx=3), dev(dy=1), dev(dy=3), dev(other=True)]
+    peers += [dev(dx=d) for d in range(1, NX)] + [dev(dy=d) for d in range(1, NY)]
+    peers += [dev(other=True)]
     for peer in peers:
         pl.semaphore_signal(barrier, inc=1, device_id=peer, device_id_type=MESH)
 
@@ -163,7 +164,7 @@
         named = jnp.broadcast_to(jnp.sum(named, axis=0, keepdims=True), (128, 128))
         gds[:, 128 * k:128 * k + 128] = jnp.transpose(named)
     gain = gainv[...].astype(F32)
-    gainf[...] = gain
+    gainf[0:56, :] = gain
     gain = jnp.concatenate([gainf[pl.ds(t, 8, stride=7), :] for t in range(7)], axis=1)
     for k in range(4):
         gainp[8 * k:8 * k + 8, :] = jnp.concatenate(
@@ -217,6 +218,8 @@
             step = 1 if c in (0, 2) else 3
             part = both(g) if c < 2 else forward(g, c - 2)
             shift = {0: 0, 1: 0, 2: 3, 3: 1}[c]
+            if j == 4 and c == 2:
+                step, part, shift = 2, both(g), 0
             if j == 4:
                 ref = region(g, me1 + shift, me2, part)
                 along_x = x_first(g)
@@ -234,21 +237,23 @@
             return (i1, i2) if x_first(g) else (i2, i1)
 
         def launch(g, j):
-            copy(g, j, 0).start()
-            copy(g, j, 1).start()
+            for c in range(3 if j == 4 else 2):
+                copy(g, j, c).start()
 
         def pass_on(g, j):
             for c in range(2):
                 copy(g, j, c).wait_recv()
-                copy(g, j, c + 2).start()
                 if j == 4:
                     launch(g, 1 + c)
+                else:
+                    copy(g, j, c + 2).start()
 
         def far(g, j):
             copy(g, j, 2).wait_recv()
-            copy(g, j, 3).wait_recv()
             if j == 4:
                 launch(g, 3)
+            else:
+                copy(g, j, 3).wait_recv()
 
         def stage(g, n):
             if n == 0:
@@ -273,7 +278,10 @@
                 far(g, 3)
 
         def copies(groups):
-            return [copy(g, j, c) for g in range(groups) for j in range(5) for c in range(4)]
+            return [
+                copy(g, j, c)
+                for g in range(groups) for j in range(5) for c in range(4) if j + c < 7
+            ]
 
         return stage, place, copies
 
@@ -366,6 +374,9 @@
 
     for d in range(1, NZ):
         state_copy(d).start()
+    for c in drains:
+        c.wait_send()
+    drains = []
     drains += [state_copy(d) for d in range(1, NZ)]
     for d in range(1, NZ):
         state_copy(d).wait_recv()
@@ -447,9 +458,30 @@
 
         return begin, middle, end, [copy(c) for c in range(6)]
 
+    def direct(g, along_x, p_ref, r_ref, send, recv):
+        me = x if along_x else y
+
+        def copy(d):
+            target = dev(dx=d) if along_x else dev(dy=d)
+            src = p_ref.at[g, lax.rem(me + d, 4)]
+            return remote(src, r_ref.at[g, d - 1], send.at[g, d - 1], recv.at[g, d - 1], target)
+
+        def begin():
+            for d in (2, 1, 3):
+                copy(d).start()
+
+        def end():
+            total = p_ref[g, me].astype(F32)
+            for d in range(1, 4):
+                copy(d).wait_recv()
+                total = total + r_ref[g, d - 1].astype(F32)
+            return total
+
+        return begin, end, [copy(d) for d in range(1, 4)]
+
     groups = range(4)
     first = [scatterer(g, g % 2 == 0, p1, m1, r1, hsend, hrecv) for g in groups]
-    second = [scatterer(g, g % 2 == 1, p2, m2, r2, ssend, srecv) for g in groups]
+    second = [direct(g, g % 2 == 1, p2, r2, ssend, srecv) for g in groups]
     for g in groups:
         base = (g % 2) * HALF + (g // 2) * WIDE
         for c in range(7):
@@ -464,12 +496,10 @@
             p2[g, i] = joined[4 * i:4 * i + 4].astype(p2.dtype)
         second[g][0]()
     for g in groups:
-        second[g][1]()
-    for g in groups:
-        joined = second[g][2]()
+        joined = second[g][1]()
         for i in range(2):
             z3s[(g % 2) * 4 + (g // 2) * 2 + i] = joined[:, 896 * i:896 * i + 896].astype(z3s.dtype)
-        drains += first[g][3] + second[g][3]
+        drains += first[g][3] + second[g][2]
 
     def last_copy(d):
         zz = lax.rem(z + d, NZ)
@@ -496,7 +526,7 @@
         last_copy(d).wait_recv()
     for b in range(NZ):
         result = result + z3r[b].astype(F32)
-    out_ref[...] = result.astype(BF)
+    out_ref[...] = result
     for c in drains:
         c.wait_send()
 
@@ -518,22 +548,22 @@
         vmem((4, 128, 512), BF), vmem((8, 128), F32), vmem((8, 8, 128), F32),
         vmem((4, 4, 16, 512), BF), vmem((2, 4, 16, 512), BF), vmem((2, 4, 16, 256), BF),
         vmem((2, 4, 16, 512), BF), vmem((128, 128), F32), vmem((4, 4, 4, 16, 512), BF),
-        vmem((4, 1536, 128), F32), vmem((8, 128), F32), vmem((2, 64, 256), BF),
+        vmem((4, 1568, 128), F32), vmem((8, 128), F32), vmem((2, 64, 256), BF),
         vmem((8, 16, 256), BF), vmem((4, 4, 4, 32, 256), BF), vmem((128, 256), F32),
         vmem((64, 256), F32), vmem((64, 256), F32), vmem((64, 256), F32),
         vmem((4, 4, 16, WIDE), BF), vmem((4, 2, 16, PART), BF), vmem((4, 2, 16, WIDE), BF),
-        vmem((4, 4, 4, WIDE), BF), vmem((4, 2, 4, PART), BF), vmem((4, 2, 4, WIDE), BF),
-        vmem((8, 4, 896), BF), vmem((8, 4, 896), BF), vmem((56, 128), F32),
+        vmem((4, 4, 4, WIDE), BF), vmem((4, 3, 4, WIDE), BF),
+        vmem((8, 4, 896), BF), vmem((8, 4, 896), BF), vmem((64, 128), F32),
         vmem((32, 256), F32), vmem((128, 256), F32),
         dma((24,)), dma((5,)), dma((5,)), dma((5, 8)), dma((5, 8)),
         dma((2, 5, 4)), dma((2, 5, 4)), dma((7,)), dma((7,)), dma((2, 5, 4)), dma((2, 5, 4)),
         dma((7,)), dma((7,)),
-        dma((4, 6)), dma((4, 6)), dma((4, 6)), dma((4, 6)),
+        dma((4, 6)), dma((4, 6)), dma((4, 3)), dma((4, 3)),
         dma((7,)), dma((7,)),
     ]
     return pl.pallas_call(
         kernel,
-        out_shape=jax.ShapeDtypeStruct((4, 896), BF),
+        out_shape=jax.ShapeDtypeStruct((4, 896), F32),
         in_specs=specs,
         out_specs=pl.BlockSpec(memory_space=pltpu.VMEM),
         scratch_shapes=scratch,
@@ -545,7 +575,7 @@
         hidden_in.T, norm_gain.reshape(56, 128),
         w_gate.reshape(32, 224, 128), w_up.reshape(32, 224, 128), w_down.reshape(128, 7168),
         expert_ids.T, gate_weights.T,
-    )
+    ).astype(BF)
 
 
 def solution(mesh):

time: 89.7 us -> 85.8 us (0.957)
  Pallas kernels: 88.2 us -> 83.5 us
  other arithmetic: 0 us -> 1.31 us
  local copies, waits for them, and re-layouts: 1.29 us -> 0 us
    pallas_call x1, Pallas kernels: 88.2 us -> 83.5 us  [per_device(): pl.pallas_call(kernel, out_shape=jax.ShapeDtypeStruct((4, 896), F32), in_...]
    convert_element_type x0 -> x1, other arithmetic: none -> 1.31 us  [per_device(): return pl.pallas_call(kernel, out_shape=jax.ShapeDtypeStruct((4, 896), F3...]
    unnamed x1 -> x0, local copies, waits for them, and re-layouts: 1.29 us -> none
where the time goes in v4:
time: 85.8 us; the launch traced here: 84.8 us
  Pallas kernels  83.5 us (97%)
  other arithmetic  1.31 us (2%)
    pallas_call x1, Pallas kernels, per_device(): pl.pallas_call(kernel, out_shape=jax.ShapeDtypeStruct((4, 896), F32), in_...  83.5 us

profile of v4, /device:TPU:32, one launch (start us, length us, event | category | flops | bytes accessed | tf_op | source)
XLA Modules:
  0.0 84.8 jit_solution(12025623858558969122)
XLA Ops:
  0.0 83.5 %shard_map.127 = f32[4,896]{1,0:T(4,128)} custom-call(bf16[4,128,512]{2,1,0:T(8,128)(2,1)} %q_hbm.1, bf16[4,64,128]{2,1,0:T(8,128)(2,1)} %qr_hbm.1, bf16[4,512,512]{2,1,0:T(8,128)(2,1)} %kc_hbm.1, bf16[4,64,512]{2,1,0:T(8,128)(2,1)} %kr_hbm.1, s32[4]{0:T(128)} %len_ref.1, bf16[16,224,512]{2,1,0:T(8,128)(2,1)} %bitcast.8, bf16[224,128]{1,0:T(8,128)(2,1)} %bitcast.12, ...), custom_call_target="tpu_custom_call" | custom-call | tf_op jit(solution)/shard_map/pallas_call | solution.py:564
  83.5 1.3 %convert_element_type.3 = bf16[4,896]{1,0:T(4,128)(2,1)} convert(f32[4,896]{1,0:T(4,128)} %shard_map.127) | non-fusion elementwise | flops 3584 | bytes 21504 | tf_op jit(solution)/shard_map/convert_element_type | solution.py:578

commit v5 on v4

--- a/solution.py
+++ b/solution.py
@@ -218,7 +218,7 @@
             step = 1 if c in (0, 2) else 3
             part = both(g) if c < 2 else forward(g, c - 2)
             shift = {0: 0, 1: 0, 2: 3, 3: 1}[c]
-            if j == 4 and c == 2:
+            if j >= 3 and c == 2:
                 step, part, shift = 2, both(g), 0
             if j == 4:
                 ref = region(g, me1 + shift, me2, part)
@@ -237,7 +237,7 @@
             return (i1, i2) if x_first(g) else (i2, i1)
 
         def launch(g, j):
-            for c in range(3 if j == 4 else 2):
+            for c in range(3 if j >= 3 else 2):
                 copy(g, j, c).start()
 
         def pass_on(g, j):
@@ -245,14 +245,14 @@
                 copy(g, j, c).wait_recv()
                 if j == 4:
                     launch(g, 1 + c)
-                else:
+                elif j < 3:
                     copy(g, j, c + 2).start()
 
         def far(g, j):
             copy(g, j, 2).wait_recv()
             if j == 4:
                 launch(g, 3)
-            else:
+            elif j < 3:
                 copy(g, j, 3).wait_recv()
 
         def stage(g, n):
@@ -280,7 +280,7 @@
         def copies(groups):
             return [
                 copy(g, j, c)
-                for g in range(groups) for j in range(5) for c in range(4) if j + c < 7
+                for g in range(groups) for j in range(5) for c in range(4) if j < 3 or c < 3
             ]
 
         return stage, place, copies

time: 85.8 us -> 81.6 us (0.951)
  Pallas kernels: 83.5 us -> 79.7 us
    pallas_call x1, Pallas kernels: 83.5 us -> 79.7 us  [per_device(): pl.pallas_call(kernel, out_shape=jax.ShapeDtypeStruct((4, 896), F32), in_...]
where the time goes in v5:
time: 81.6 us; the launch traced here: 81 us
  Pallas kernels  79.7 us (98%)
  other arithmetic  1.31 us (2%)
    pallas_call x1, Pallas kernels, per_device(): pl.pallas_call(kernel, out_shape=jax.ShapeDtypeStruct((4, 896), F32), in_...  79.7 us

profile of v5, /device:TPU:32, one launch (start us, length us, event | category | flops | bytes accessed | tf_op | source)
XLA Modules:
  0.0 81.0 jit_solution(17609321711699302106)
XLA Ops:
  0.0 79.7 %shard_map.127 = f32[4,896]{1,0:T(4,128)} custom-call(bf16[4,128,512]{2,1,0:T(8,128)(2,1)} %q_hbm.1, bf16[4,64,128]{2,1,0:T(8,128)(2,1)} %qr_hbm.1, bf16[4,512,512]{2,1,0:T(8,128)(2,1)} %kc_hbm.1, bf16[4,64,512]{2,1,0:T(8,128)(2,1)} %kr_hbm.1, s32[4]{0:T(128)} %len_ref.1, bf16[16,224,512]{2,1,0:T(8,128)(2,1)} %bitcast.8, bf16[224,128]{1,0:T(8,128)(2,1)} %bitcast.12, ...), custom_call_target="tpu_custom_call" | custom-call | tf_op jit(solution)/shard_map/pallas_call | solution.py:564
  79.7 1.3 %convert_element_type.3 = bf16[4,896]{1,0:T(4,128)(2,1)} convert(f32[4,896]{1,0:T(4,128)} %shard_map.127) | non-fusion elementwise | flops 3584 | bytes 21504 | tf_op jit(solution)/shard_map/convert_element_type | solution.py:578
